TPU v7x, 32 devices: a whole 2x2x4 slice. The times are simulated.
32 devices in a mesh: rows: 4 (over y, x), cols: 8 (over z, core).
Axes of the slice: x: 2, y: 2, z: 4, core: 2. Of those that a mesh axis runs over, the one named last changes fastest.
Arguments:
- latent1: bfloat16 [64, 512, 320], P('rows', 'cols'), may hold values from -15 to 15, as said below
- norm1a_g: float32 [320], replicated, may hold values from 0.25 to 1.75
- norm1a_b: float32 [320], replicated, may hold values from -3 to 3
- conv1a_w: bfloat16 [3, 3, 320, 320], replicated, may hold values from -0.109375 to 0.109375
- norm1b_g: float32 [320], replicated, may hold values from 0.25 to 1.75
- norm1b_b: float32 [320], replicated, may hold values from -3 to 3
- conv1b_w: bfloat16 [3, 3, 320, 320], replicated, may hold values from -0.109375 to 0.109375
- conv1b_b: float32 [320], replicated, may hold values from -3 to 3
- feat3: bfloat16 [16, 128, 1280], P('rows', 'cols'), may hold values from -15 to 15, as said below
- adapter3: bfloat16 [16, 128, 1280], P('rows', 'cols'), may hold values from -15 to 15, as said below
- norm3a_g: float32 [1280], replicated, may hold values from 0.25 to 1.75
- norm3a_b: float32 [1280], replicated, may hold values from -3 to 3
- conv3a_w: bfloat16 [3, 3, 1280, 1280], P(None, None, None, 'cols'), may hold values from -0.0546875 to 0.0546875
- norm3b_g: float32 [1280], P('cols'), may hold values from 0.25 to 1.75
- norm3b_b: float32 [1280], P('cols'), may hold values from -3 to 3
- conv3b_w: bfloat16 [3, 3, 1280, 1280], P(None, None, None, 'cols'), may hold values from -0.0546875 to 0.0546875
- conv3b_b: float32 [1280], P('cols'), may hold values from -3 to 3
Outputs:
- out1: bfloat16 [64, 512, 320], P('rows', 'cols')
- out3: bfloat16 [16, 128, 1280], P('rows', None, 'cols')
Inputs may be any that keep to these rules, and one draw needn't show every extreme that they name: `latent1`: real values. `feat3`: real values. `adapter3`: real values.
All inputs are finite; a program needn't handle non-finite values.
Results may differ from a plain program's by a relative error of at most 0.0052.
Values may be sent and summed in bfloat16 or wider, within the bound.
No kernel may reach another device: no remote copies, remote signals or barrier semaphores. Data moves between devices by JAX's collectives and lax.ppermute only.
A program may use at most 128 MiB of HBM per device.

v0:
```python
import jax
import jax.numpy as jnp
from jax import lax
from jax.sharding import PartitionSpec as P

C1 = 320
C3 = 1280
norm_eps = 1e-05


def extended(block, sides, width):
    for axis, dim in sides:
        count = lax.axis_size(axis)
        forward = [(i, i + 1) for i in range(count - 1)]
        backward = [(target, source) for source, target in forward]
        low = lax.ppermute(
            lax.slice_in_dim(block, block.shape[dim] - width, None, axis=dim), axis, forward
        )
        high = lax.ppermute(lax.slice_in_dim(block, 0, width, axis=dim), axis, backward)
        block = jnp.concatenate([low, block, high], axis=dim)
    return block


def conv_valid(padded, kernel):
    return lax.conv_general_dilated(
        padded[None],
        kernel,
        (1, 1),
        "VALID",
        dimension_numbers=("NHWC", "HWIO", "NHWC"),
        preferred_element_type=jnp.float32,
    )[0]


def moments(value, group_width):
    height, width, chans = value.shape
    grouped = value.astype(jnp.float32).reshape(height, width, chans // group_width, group_width)
    return (jnp.sum(grouped, axis=(0, 1, 3)), jnp.sum(grouped * grouped, axis=(0, 1, 3)))


def normalize(value, sums, squares, count, gain, shift):
    height, width, chans = value.shape
    groups = sums.shape[0]
    mean = sums / count
    inverse = lax.rsqrt(squares / count - mean * mean + norm_eps)
    grouped = value.astype(jnp.float32).reshape(height, width, groups, chans // groups)
    normed = ((grouped - mean[:, None]) * inverse[:, None]).reshape(height, width, chans)
    return jax.nn.silu(normed * gain + shift).astype(jnp.bfloat16)


def level3_totals(values, group_width):
    sums, squares = moments(values, group_width)
    return lax.psum((sums, squares), "rows")


def folder(kernel, total, piece):
    height = total.shape[0]
    width = total.shape[1]
    count = piece.shape[2]
    wide = jnp.pad(piece, ((0, 0), (1, 1), (0, 0)))
    taps = [wide[dy : dy + height, dx : dx + width, :] for dy in range(3) for dx in range(3)]
    patches = jnp.concatenate(taps, axis=2).reshape(height * width, 9 * count)
    weights = kernel.reshape(9 * count, kernel.shape[3])
    product = jnp.dot(patches, weights, preferred_element_type=jnp.float32)
    return product.reshape(height, width, kernel.shape[3])


def body(
    latent1,
    norm1a_g,
    norm1a_b,
    conv1a_w,
    norm1b_g,
    norm1b_b,
    conv1b_w,
    conv1b_b,
    feat3,
    adapter3,
    norm3a_g,
    norm3a_b,
    conv3a_w,
    norm3b_g,
    norm3b_b,
    conv3b_w,
    conv3b_b,
):
    rows_one = latent1.shape[0]
    cols_one = latent1.shape[1]
    width_one = C1 // 32
    count_one = rows_one * cols_one * lax.axis_size("rows") * lax.axis_size("cols") * width_one
    sums, squares = moments(latent1, width_one)
    sums, squares = lax.psum((sums, squares), ("rows", "cols"))
    act1 = normalize(latent1, sums, squares, count_one, norm1a_g, norm1a_b)
    padded = extended(act1, (("rows", 0), ("cols", 1)), 1)
    hid1 = conv_valid(padded, conv1a_w)
    sums_two, squares_two = moments(hid1, width_one)
    sums_two, squares_two = lax.psum((sums_two, squares_two), ("rows", "cols"))
    act2 = normalize(hid1, sums_two, squares_two, count_one, norm1b_g, norm1b_b)
    padded_two = extended(act2, (("rows", 0), ("cols", 1)), 1)
    out1 = (latent1.astype(jnp.float32) + conv_valid(padded_two, conv1b_w) + conv1b_b).astype(
        jnp.bfloat16
    )
    joined = (feat3.astype(jnp.float32) + adapter3.astype(jnp.float32)).astype(jnp.bfloat16)
    shard = conv3a_w.shape[3]
    height = feat3.shape[0]
    width = feat3.shape[1] * lax.axis_size("cols")
    width_three = C3 // 32
    count_three = height * width * lax.axis_size("rows") * width_three
    empty = jnp.zeros((height, width, shard), jnp.float32)
    edged_tile = extended(joined, (("rows", 0),), 1)
    whole = lax.all_gather(edged_tile, "cols", axis=1, tiled=True)
    local = lax.dynamic_slice_in_dim(whole[1:-1], lax.axis_index("cols") * shard, shard, 2)
    sums_three, squares_three = level3_totals(whole[1:-1], width_three)
    line_ids = lax.axis_index("rows") * height - 1 + jnp.arange(height + 2, dtype=jnp.int32)
    line_ok = (line_ids >= 0) & (line_ids < height * lax.axis_size("rows"))
    act_whole = normalize(whole, sums_three, squares_three, count_three, norm3a_g, norm3a_b)
    act_whole = jnp.where(line_ok[:, None, None], act_whole, jnp.zeros((), jnp.bfloat16))
    hid3 = conv_valid(jnp.pad(act_whole, ((0, 0), (1, 1), (0, 0))), conv3a_w)
    sums_four, squares_four = moments(hid3, width_three)
    sums_four, squares_four = lax.psum((sums_four, squares_four), "rows")
    act4 = normalize(hid3, sums_four, squares_four, count_three, norm3b_g, norm3b_b)
    edged_two = extended(act4, (("rows", 0),), 1)
    second = folder(conv3b_w, empty, lax.all_gather(edged_two, "cols", axis=2, tiled=True))
    out3 = (local.astype(jnp.float32) + second + conv3b_b).astype(jnp.bfloat16)
    return (out1, out3)


def solution(mesh):
    placed = (
        P("rows", "cols", None),
        P(),
        P(),
        P(),
        P(),
        P(),
        P(),
        P(),
        P("rows", "cols", None),
        P("rows", "cols", None),
        P(),
        P(),
        P(None, None, None, "cols"),
        P("cols"),
        P("cols"),
        P(None, None, None, "cols"),
        P("cols"),
    )
    return jax.shard_map(
        body,
        mesh=mesh,
        in_specs=placed,
        out_specs=(P("rows", "cols", None), P("rows", None, "cols")),
        check_vma=False,
    )
```

profile of v0, /device:TPU:3, one launch (start us, length us, event | category | flops | bytes accessed | tf_op | source)
XLA Modules:
  0.0 271.7 jit_solution(1989159942951387046)
XLA Ops:
  7.2 1.2 add_convert_fusion
  8.4 3.1 %collective-permute-start.8 = (bf16[1,16,1280]{2,1,0:T(8,128)(2,1)S(1)}, bf16[1,16,1280]{2,1,0:T(8,128)(2,1)S(1)}, u32[]{:S(2)}, u32[]{:S(2)}) collective-permute-start(bf16[1,16,1280]{2,1,0:T(8,128)(2,1)S(1)} %get-tuple-element.38), channel_id=1, source_target_pairs={{0,8},{8,16},{16,24},{1,9},{9,17},{17,25},{2,10},{10,18},{18,26},{... | collective-permute-start | bytes 122888 | tf_op jit(solution)/shard_map/ppermute | solution.py:16
  11.6 2.2 collective-permute-start.9
  13.7 3.5 %collective-permute-done.9 = bf16[1,16,1280]{2,1,0:T(8,128)(2,1)S(1)} collective-permute-done((bf16[1,16,1280]{2,1,0:T(8,128)(2,1)S(1)}, bf16[1,16,1280]{2,1,0:T(8,128)(2,1)S(1)}, u32[]{:S(2)}, u32[]{:S(2)}) %collective-permute-start.9) | collective-permute-done | bytes 40992 | tf_op jit(solution)/shard_map/ppermute | solution.py:19
  17.2 0.7 pad_maximum_fusion
  18.0 1.6 convert_reduce_fusion.1
  19.8 0.6 reduce_sum.100
  20.5 0.7 reduce_sum.97
  21.2 27.1 %all-gather.3.cloned.1.call-done = bf16[6,128,1280]{2,1,0:T(8,128)(2,1)} async-done(((bf16[6,16,1280]{2,1,0:T(8,128)(2,1)}), bf16[6,128,1280]{2,1,0:T(8,128)(2,1)}) %all-gather.3.cloned.1.call-update) | async-done | bytes 1966096 | tf_op jit(solution)/shard_map/all_gather | solution.py:111
  48.3 1.3 slice-done
  49.6 1.4 copy.113
  51.0 1.8 convert_reduce_fusion
  53.2 6.0 %all-reduce.5 = (f32[32]{0:T(128)S(1)}, f32[32]{0:T(128)S(1)}) all-reduce(f32[32]{0:T(128)S(1)} %reduce_sum.145, f32[32]{0:T(128)S(1)} %reduce_sum.115), channel_id=1, replica_groups=mesh['rows'=4,'cols'=8] {'rows'}, use_global_device_ids=true, to_apply=%region_17.18 | all-reduce | flops 64 | bytes 512 | tf_op jit(solution)/shard_map/psum | solution.py:53
  59.5 3.0 %fusion.11 = bf16[6,128,1280]{2,1,0:T(8,128)(2,1)S(1)} fusion(bf16[6,128,1280]{2,1,0:T(8,128)(2,1)} %all-gather.3.cloned.1.call-done, f32[1280]{0:T(1024)S(1)} %copy-done.4, f32[1280]{0:T(1024)S(1)} %copy-done.5, f32[1280]{0:T(1024)S(1)} %mul.156, f32[1280]{0:T(1024)S(1)} %sub.79, pred[6]{0:T(512)(128)(4,1)S(1)} %compare_and_fusion), kind=kLoop, calls=%fused_computation.20 | loop fusion | flops 10813440 | bytes 3952646 | tf_op jit(solution)/shard_map/jit(_where)/select_n | solution.py:117
  62.6 0.5 pad_bitcast_fusion
  63.0 1.5 pad.13
  64.5 4.2 %reshape.81 = bf16[6,1,8,17,1280]{4,3,2,0,1:T(8,128)(2,1)} reshape(bf16[6,1,136,1280]{3,2,0,1:T(8,128)(2,1)} %pad.13) | data formatting | bytes 4177920 | tf_op jit(solution)/shard_map/conv_general_dilated | solution.py:25
  68.7 2.4 copy.104
  71.1 0.5 copy-done.15
  71.6 3.5 %select_reduce_fusion.3 = (f32[160]{0:T(256)S(1)}, f32[160]{0:T(256)S(1)}, f32[4,8,17,160]{3,1,2,0:T(8,128)S(1)}) fusion(pred[8,17]{0,1:T(8,128)(4,1)S(1)} %copy-done.18, bf16[3,3,1280,160]{2,3,1,0:T(8,128)(2,1)S(1)} %copy-done.15, bf16[6,1,7,2,1280]{4,2,3,0,1:T(8,128)(2,1)S(1)} %slice.109, bf16[6,1,8,17,1280]{4,2,3,0,1:T(8,128)(2,1)S(1)} %copy.104), kind=kOutput, calls=%fused_computation.73 | convolution fusion | flops 2012927744 | bytes 6339976 | tf_op jit(solution)/shard_map/conv_general_dilated | solution.py:25
  75.5 42.0 %all-reduce.3 = (f32[32]{0:T(128)}, f32[32]{0:T(128)}) all-reduce(f32[32]{0:T(128)S(1)} %copy-done.11, f32[32]{0:T(128)S(1)} %copy-done.12), channel_id=1, replica_groups=mesh['rows'=4,'cols'=8] {'rows','cols'}, use_global_device_ids=true, to_apply=%region_5.6 | all-reduce | flops 64 | bytes 512 | tf_op jit(solution)/shard_map/psum | solution.py:92
  117.5 6.0 %all-reduce.4 = (f32[4]{0:T(128)S(1)}, f32[4]{0:T(128)S(1)}) all-reduce(f32[4]{0:T(128)S(1)} %reduce_sum.151, f32[4]{0:T(128)S(1)} %reduce_sum.148), channel_id=1, replica_groups=mesh['rows'=4,'cols'=8] {'rows'}, use_global_device_ids=true, to_apply=%region_23.24 | all-reduce | flops 8 | bytes 64 | tf_op jit(solution)/shard_map/psum | solution.py:120
  123.6 0.7 mul.165
  124.3 0.7 sub.84
  125.3 0.9 copy.114
  126.3 1.2 multiply_convert_fusion.2
  127.5 4.0 %collective-permute-start.10 = (bf16[1,128,160]{1,2,0:T(8,128)(2,1)S(1)}, bf16[1,128,160]{1,2,0:T(8,128)(2,1)S(1)}, u32[]{:S(2)}, u32[]{:S(2)}) collective-permute-start(bf16[1,128,160]{1,2,0:T(8,128)(2,1)S(1)} %get-tuple-element.36), channel_id=1, source_target_pairs={{0,8},{8,16},{16,24},{1,9},{9,17},{17,25},{2,10},{10,18},{18,26},{... | collective-permute-start | bytes 122888 | tf_op jit(solution)/shard_map/ppermute | solution.py:16
  131.5 1.9 collective-permute-start.11
  133.8 3.3 %collective-permute-done.11 = bf16[1,128,160]{1,2,0:T(8,128)(2,1)S(1)} collective-permute-done((bf16[1,128,160]{1,2,0:T(8,128)(2,1)S(1)}, bf16[1,128,160]{1,2,0:T(8,128)(2,1)S(1)}, u32[]{:S(2)}, u32[]{:S(2)}) %collective-permute-start.11) | collective-permute-done | bytes 40992 | tf_op jit(solution)/shard_map/ppermute | solution.py:19
  137.1 0.7 pad_maximum_fusion.1
  137.9 0.8 fusion.20
  138.8 1.9 collective-permute-start
  140.8 3.4 %collective-permute-start.1 = (bf16[1,64,320]{2,0,1:T(2,128)(2,1)S(1)}, bf16[1,64,320]{2,0,1:T(2,128)(2,1)S(1)}, u32[]{:S(2)}, u32[]{:S(2)}) collective-permute-start(bf16[1,64,320]{2,0,1:T(2,128)(2,1)S(1)} %get-tuple-element.35), channel_id=1, source_target_pairs={{8,0},{16,8},{24,16},{9,1},{17,9},{25,17},{10,2},{18,10},{26,18},{... | collective-permute-start | bytes 122888 | tf_op jit(solution)/shard_map/ppermute | solution.py:19
  144.2 2.8 %collective-permute-done.1 = bf16[1,64,320]{2,0,1:T(2,128)(2,1)S(1)} collective-permute-done((bf16[1,64,320]{2,0,1:T(2,128)(2,1)S(1)}, bf16[1,64,320]{2,0,1:T(2,128)(2,1)S(1)}, u32[]{:S(2)}, u32[]{:S(2)}) %collective-permute-start.1) | collective-permute-done | bytes 40992 | tf_op jit(solution)/shard_map/ppermute | solution.py:19
  147.0 9.3 %collective-permute-start.2 = (bf16[18,1,320]{2,0,1:T(8,128)(2,1)S(1)}, bf16[18,1,320]{2,0,1:T(8,128)(2,1)S(1)}, u32[]{:S(2)}, u32[]{:S(2)}) collective-permute-start(bf16[18,1,320]{2,0,1:T(8,128)(2,1)S(1)} %get-tuple-element.30), channel_id=1, source_target_pairs={{0,1},{1,2},{2,3},{3,4},{4,5},{5,6},{6,7},{8,9},{9,10},{10,11},{11... | collective-permute-start | bytes 34568 | tf_op jit(solution)/shard_map/ppermute | solution.py:16
  156.3 2.1 collective-permute-start.3
  158.4 4.4 %collective-permute-done.3 = bf16[18,1,320]{2,0,1:T(8,128)(2,1)S(1)} collective-permute-done((bf16[18,1,320]{2,0,1:T(8,128)(2,1)S(1)}, bf16[18,1,320]{2,0,1:T(8,128)(2,1)S(1)}, u32[]{:S(2)}, u32[]{:S(2)}) %collective-permute-start.3) | collective-permute-done | bytes 11552 | tf_op jit(solution)/shard_map/ppermute | solution.py:19
  162.8 0.7 maximum_bitcast_fusion
  164.2 5.1 %select_reduce_fusion.1 = (f32[320]{0:T(512)S(1)}, f32[320]{0:T(512)S(1)}, f32[16,8,9,320]{3,1,2,0:T(8,128)}) fusion(pred[8,9]{0,1:T(8,128)(4,1)S(1)} %copy-done.19, bf16[3,3,320,320]{3,2,1,0:T(8,128)(2,1)S(1)} %copy-done, bf16[18,1,7,2,320]{4,2,3,0,1:T(8,128)(2,1)S(1)} %slice.100, bf16[18,1,8,9,320]{4,2,3,0,1:T(8,128)(2,1)S(1)} %copy.97), kind=kOutput, calls=%fused_computation.22 | convolution fusion | flops 2128619008 | bytes 4311112 | tf_op jit(solution)/shard_map/conv_general_dilated | solution.py:25
  169.8 37.3 %all-reduce.2 = (f32[32]{0:T(128)S(1)}, f32[32]{0:T(128)S(1)}) all-reduce(f32[32]{0:T(128)S(1)} %reduce_sum.112, f32[32]{0:T(128)S(1)} %reduce_sum.106), channel_id=1, replica_groups=mesh['rows'=4,'cols'=8] {'rows','cols'}, use_global_device_ids=true, to_apply=%region_11.12 | all-reduce | flops 64 | bytes 512 | tf_op jit(solution)/shard_map/psum | solution.py:97
  207.5 1.8 copy.98
  209.3 0.5 multiply_convert_fusion.1
  210.0 3.1 %collective-permute-start.4 = (bf16[1,64,320]{2,0,1:T(2,128)(2,1)S(1)}, bf16[1,64,320]{2,0,1:T(2,128)(2,1)S(1)}, u32[]{:S(2)}, u32[]{:S(2)}) collective-permute-start(bf16[1,64,320]{2,0,1:T(2,128)(2,1)S(1)} %get-tuple-element.32), channel_id=1, source_target_pairs={{0,8},{8,16},{16,24},{1,9},{9,17},{17,25},{2,10},{10,18},{18,26},{... | collective-permute-start | bytes 122888 | tf_op jit(solution)/shard_map/ppermute | solution.py:16
  213.1 2.2 collective-permute-start.5
  215.4 4.0 %collective-permute-done.5 = bf16[1,64,320]{2,0,1:T(2,128)(2,1)S(1)} collective-permute-done((bf16[1,64,320]{2,0,1:T(2,128)(2,1)S(1)}, bf16[1,64,320]{2,0,1:T(2,128)(2,1)S(1)}, u32[]{:S(2)}, u32[]{:S(2)}) %collective-permute-start.5) | collective-permute-done | bytes 40992 | tf_op jit(solution)/shard_map/ppermute | solution.py:19
  219.4 6.1 %collective-permute-start.6 = (bf16[18,1,320]{2,0,1:T(8,128)(2,1)S(1)}, bf16[18,1,320]{2,0,1:T(8,128)(2,1)S(1)}, u32[]{:S(2)}, u32[]{:S(2)}) collective-permute-start(bf16[18,1,320]{2,0,1:T(8,128)(2,1)S(1)} %get-tuple-element.28), channel_id=1, source_target_pairs={{0,1},{1,2},{2,3},{3,4},{4,5},{5,6},{6,7},{8,9},{9,10},{10,11},{11... | collective-permute-start | bytes 34568 | tf_op jit(solution)/shard_map/ppermute | solution.py:16
  225.5 1.9 collective-permute-start.7
  227.5 7.4 %copy.111 = bf16[3,3,1280,160]{2,1,0,3:T(4,128)(2,1)} copy(bf16[3,3,1280,160]{2,3,1,0:T(8,128)(2,1)} %param.32) | data formatting | bytes 7372800 | tf_op args[15]
  234.9 9.4 %reshape.109 = bf16[11520,160,1]{0,1,2:T(8,128)(2,1)} reshape(bf16[3,3,1280,160]{2,1,0,3:T(4,128)(2,1)} %copy.111) | data formatting | bytes 7372800 | tf_op jit(solution)/shard_map/reshape | solution.py:63
  244.3 0.7 maximum_bitcast_fusion.1
  245.4 1.2 copy-done.16
  246.6 3.8 %convolution_select_fusion = f32[16,8,9,320]{3,1,2,0:T(8,128)S(1)} fusion(bf16[3,3,320,320]{3,2,1,0:T(8,128)(2,1)S(1)} %copy-done.16, bf16[18,1,7,2,320]{4,2,3,0,1:T(8,128)(2,1)S(1)} %slice.104, bf16[18,1,8,9,320]{4,2,3,0,1:T(8,128)(2,1)S(1)} %copy.100, pred[8,9]{0,1:T(8,128)(4,1)S(1)} %copy-done.19), kind=kOutput, calls=%fused_computation.42 | convolution fusion | flops 2126776320 | bytes 4308552 | tf_op jit(solution)/shard_map/conv_general_dilated | solution.py:25
  250.5 0.3 copy.101
  250.8 0.3 copy-done.10
  251.1 0.5 fusion.23
  251.7 1.1 copy.112
  252.8 2.7 copy.107
  255.8 0.3 slice_dynamic-update-slice_fusion.7
  256.1 0.3 slice_dynamic-update-slice_fusion.6
  256.5 0.3 slice_dynamic-update-slice_fusion.5
  256.9 0.3 slice_dynamic-update-slice_fusion.4
  257.3 0.3 slice_dynamic-update-slice_fusion.3
  257.6 1.6 copy-done.3
  259.2 5.7 %fusion.45 = bf16[4,128,160]{1,2,0:T(8,128)(2,1)} fusion(bf16[4,128,11520]{2,1,0:T(8,128)(2,1)S(1)} %slice_dynamic-update-slice_fusion.3, bf16[11520,160,1]{0,1,2:T(8,128)(2,1)S(1)} %copy-done.3, f32[160]{0:T(256)S(1)} %copy-done.17, bf16[4,128,1280]{1,2,0:T(8,128)(2,1)} %copy.113, s32[]{:T(128)S(6)} %select_n.7), kind=kOutput, calls=%fused_computation.69 | convolution fusion | flops 1887764480 | bytes 15811204 | tf_op jit(solution)/shard_map/dot_general | solution.py:64
  (101 shorter events, 5.2 us)
Async XLA Ops:
  7.2 156.8 %copy-start = (bf16[3,3,320,320]{3,2,1,0:T(8,128)(2,1)S(1)}, bf16[3,3,320,320]{3,2,1,0:T(8,128)(2,1)}, u32[]{:S(2)}) copy-start(bf16[3,3,320,320]{3,2,1,0:T(8,128)(2,1)} %param.20) | copy-start | bytes 5529604
  7.2 41.1 %all-gather.3.cloned.1.call-start = ((), (), s32[]{:S(2)}) async-start(), calls=%async_computation | async-start | bytes 2211840 | tf_op jit(solution)/shard_map/all_gather | solution.py:111
  8.4 5.3 %collective-permute-start.8 = (bf16[1,16,1280]{2,1,0:T(8,128)(2,1)S(1)}, bf16[1,16,1280]{2,1,0:T(8,128)(2,1)S(1)}, u32[]{:S(2)}, u32[]{:S(2)}) collective-permute-start(bf16[1,16,1280]{2,1,0:T(8,128)(2,1)S(1)} %get-tuple-element.38), channel_id=1, source_target_pairs={{0,8},{8,16},{16,24},{1,9},{9,17},{17,25},{2,10},{10,18},{18,26},{... | collective-permute-start | bytes 122888 | tf_op jit(solution)/shard_map/ppermute | solution.py:16
  11.6 5.6 %collective-permute-start.9 = (bf16[1,16,1280]{2,1,0:T(8,128)(2,1)S(1)}, bf16[1,16,1280]{2,1,0:T(8,128)(2,1)S(1)}, u32[]{:S(2)}, u32[]{:S(2)}) collective-permute-start(bf16[1,16,1280]{2,1,0:T(8,128)(2,1)S(1)} %get-tuple-element.39), channel_id=1, source_target_pairs={{8,0},{16,8},{24,16},{9,1},{17,9},{25,17},{10,2},{18,10},{26,18},{... | collective-permute-start | bytes 122888 | tf_op jit(solution)/shard_map/ppermute | solution.py:19
  17.9 234.8 %all-gather.5.cloned.1.call-start = ((), (), s32[]{:S(2)}) async-start(), calls=%async_computation.1 | async-start | bytes 2211840 | tf_op jit(solution)/shard_map/all_gather | solution.py:123
  48.3 1.3 slice-start
  49.6 9.9 %copy-start.4 = (f32[1280]{0:T(1024)S(1)}, f32[1280]{0:T(1024)}, u32[]{:S(2)}) copy-start(f32[1280]{0:T(1024)} %param.28) | copy-start | bytes 15364
  49.6 10.0 %copy-start.5 = (f32[1280]{0:T(1024)S(1)}, f32[1280]{0:T(1024)}, u32[]{:S(2)}) copy-start(f32[1280]{0:T(1024)} %param.27) | copy-start | bytes 15364
  68.7 2.9 %copy-start.15 = (bf16[3,3,1280,160]{2,3,1,0:T(8,128)(2,1)S(1)}, bf16[3,3,1280,160]{2,3,1,0:T(8,128)(2,1)}, u32[]{:S(2)}) copy-start(bf16[3,3,1280,160]{2,3,1,0:T(8,128)(2,1)} %param.29) | copy-start | bytes 11059204
  68.7 2.9 %copy-start.18 = (pred[8,17]{0,1:T(8,128)(4,1)S(1)}, pred[8,17]{0,1:T(8,128)(4,1)}, u32[]{:S(2)}) copy-start(pred[8,17]{0,1:T(8,128)(4,1)} %constant.75) | copy-start | bytes 412
  71.6 3.9 %copy-start.11 = (f32[32]{0:T(128)S(1)}, f32[32]{0:T(128)}, u32[]{:S(2)}) copy-start(f32[32]{0:T(128)} %reduce_sum.100) | copy-start | bytes 388
  71.6 3.9 %copy-start.12 = (f32[32]{0:T(128)S(1)}, f32[32]{0:T(128)}, u32[]{:S(2)}) copy-start(f32[32]{0:T(128)} %reduce_sum.97) | copy-start | bytes 388
  125.0 12.9 %copy-start.2 = (bf16[16,64,320]{2,1,0:T(8,128)(2,1)S(1)}, bf16[16,64,320]{2,1,0:T(8,128)(2,1)}, u32[]{:S(2)}) copy-start(bf16[16,64,320]{2,1,0:T(8,128)(2,1)} %param.17) | copy-start | bytes 1966084
  125.2 8.2 %copy-start.13 = (f32[32]{0:T(128)S(1)}, f32[32]{0:T(128)}, u32[]{:S(2)}) copy-start(f32[32]{0:T(128)} %get-tuple-element.22) | copy-start | bytes 388
  125.2 8.2 %copy-start.14 = (f32[32]{0:T(128)S(1)}, f32[32]{0:T(128)}, u32[]{:S(2)}) copy-start(f32[32]{0:T(128)} %get-tuple-element.23) | copy-start | bytes 388
  125.3 12.6 %copy-start.6 = (f32[320]{0:T(512)S(1)}, f32[320]{0:T(512)}, u32[]{:S(2)}) copy-start(f32[320]{0:T(512)} %param.19) | copy-start | bytes 3844
  125.3 12.6 %copy-start.7 = (f32[320]{0:T(512)S(1)}, f32[320]{0:T(512)}, u32[]{:S(2)}) copy-start(f32[320]{0:T(512)} %param.18) | copy-start | bytes 3844
  127.5 6.3 %collective-permute-start.10 = (bf16[1,128,160]{1,2,0:T(8,128)(2,1)S(1)}, bf16[1,128,160]{1,2,0:T(8,128)(2,1)S(1)}, u32[]{:S(2)}, u32[]{:S(2)}) collective-permute-start(bf16[1,128,160]{1,2,0:T(8,128)(2,1)S(1)} %get-tuple-element.36), channel_id=1, source_target_pairs={{0,8},{8,16},{16,24},{1,9},{9,17},{17,25},{2,10},{10,18},{18,26},{... | collective-permute-start | bytes 122888 | tf_op jit(solution)/shard_map/ppermute | solution.py:16
  131.5 5.6 %collective-permute-start.11 = (bf16[1,128,160]{1,2,0:T(8,128)(2,1)S(1)}, bf16[1,128,160]{1,2,0:T(8,128)(2,1)S(1)}, u32[]{:S(2)}, u32[]{:S(2)}) collective-permute-start(bf16[1,128,160]{1,2,0:T(8,128)(2,1)S(1)} %get-tuple-element.37), channel_id=1, source_target_pairs={{8,0},{16,8},{24,16},{9,1},{17,9},{25,17},{10,2},{18,10},{26,18},{... | collective-permute-start | bytes 122888 | tf_op jit(solution)/shard_map/ppermute | solution.py:19
  138.8 5.4 %collective-permute-start = (bf16[1,64,320]{2,0,1:T(2,128)(2,1)S(1)}, bf16[1,64,320]{2,0,1:T(2,128)(2,1)S(1)}, u32[]{:S(2)}, u32[]{:S(2)}) collective-permute-start(bf16[1,64,320]{2,0,1:T(2,128)(2,1)S(1)} %get-tuple-element.34), channel_id=1, source_target_pairs={{0,8},{8,16},{16,24},{1,9},{9,17},{17,25},{2,10},{10,18},{18,26},{... | collective-permute-start | bytes 122888 | tf_op jit(solution)/shard_map/ppermute | solution.py:16
  140.8 6.3 %collective-permute-start.1 = (bf16[1,64,320]{2,0,1:T(2,128)(2,1)S(1)}, bf16[1,64,320]{2,0,1:T(2,128)(2,1)S(1)}, u32[]{:S(2)}, u32[]{:S(2)}) collective-permute-start(bf16[1,64,320]{2,0,1:T(2,128)(2,1)S(1)} %get-tuple-element.35), channel_id=1, source_target_pairs={{8,0},{16,8},{24,16},{9,1},{17,9},{25,17},{10,2},{18,10},{26,18},{... | collective-permute-start | bytes 122888 | tf_op jit(solution)/shard_map/ppermute | solution.py:19
  147.0 11.4 %collective-permute-start.2 = (bf16[18,1,320]{2,0,1:T(8,128)(2,1)S(1)}, bf16[18,1,320]{2,0,1:T(8,128)(2,1)S(1)}, u32[]{:S(2)}, u32[]{:S(2)}) collective-permute-start(bf16[18,1,320]{2,0,1:T(8,128)(2,1)S(1)} %get-tuple-element.30), channel_id=1, source_target_pairs={{0,1},{1,2},{2,3},{3,4},{4,5},{5,6},{6,7},{8,9},{9,10},{10,11},{11... | collective-permute-start | bytes 34568 | tf_op jit(solution)/shard_map/ppermute | solution.py:16
  156.3 6.5 %collective-permute-start.3 = (bf16[18,1,320]{2,0,1:T(8,128)(2,1)S(1)}, bf16[18,1,320]{2,0,1:T(8,128)(2,1)S(1)}, u32[]{:S(2)}, u32[]{:S(2)}) collective-permute-start(bf16[18,1,320]{2,0,1:T(8,128)(2,1)S(1)} %get-tuple-element.31), channel_id=1, source_target_pairs={{1,0},{2,1},{3,2},{4,3},{5,4},{6,5},{7,6},{9,8},{10,9},{11,10},{12... | collective-permute-start | bytes 34568 | tf_op jit(solution)/shard_map/ppermute | solution.py:19
  163.6 0.7 copy-start.19
  169.4 39.9 %copy-start.8 = (f32[320]{0:T(512)S(1)}, f32[320]{0:T(512)}, u32[]{:S(2)}) copy-start(f32[320]{0:T(512)} %param.22) | copy-start | bytes 3844
  169.4 39.9 %copy-start.9 = (f32[320]{0:T(512)S(1)}, f32[320]{0:T(512)}, u32[]{:S(2)}) copy-start(f32[320]{0:T(512)} %param.21) | copy-start | bytes 3844
  210.0 5.4 %collective-permute-start.4 = (bf16[1,64,320]{2,0,1:T(2,128)(2,1)S(1)}, bf16[1,64,320]{2,0,1:T(2,128)(2,1)S(1)}, u32[]{:S(2)}, u32[]{:S(2)}) collective-permute-start(bf16[1,64,320]{2,0,1:T(2,128)(2,1)S(1)} %get-tuple-element.32), channel_id=1, source_target_pairs={{0,8},{8,16},{16,24},{1,9},{9,17},{17,25},{2,10},{10,18},{18,26},{... | collective-permute-start | bytes 122888 | tf_op jit(solution)/shard_map/ppermute | solution.py:16
  213.1 6.3 %collective-permute-start.5 = (bf16[1,64,320]{2,0,1:T(2,128)(2,1)S(1)}, bf16[1,64,320]{2,0,1:T(2,128)(2,1)S(1)}, u32[]{:S(2)}, u32[]{:S(2)}) collective-permute-start(bf16[1,64,320]{2,0,1:T(2,128)(2,1)S(1)} %get-tuple-element.33), channel_id=1, source_target_pairs={{8,0},{16,8},{24,16},{9,1},{17,9},{25,17},{10,2},{18,10},{26,18},{... | collective-permute-start | bytes 122888 | tf_op jit(solution)/shard_map/ppermute | solution.py:19
  219.4 24.9 %collective-permute-start.6 = (bf16[18,1,320]{2,0,1:T(8,128)(2,1)S(1)}, bf16[18,1,320]{2,0,1:T(8,128)(2,1)S(1)}, u32[]{:S(2)}, u32[]{:S(2)}) collective-permute-start(bf16[18,1,320]{2,0,1:T(8,128)(2,1)S(1)} %get-tuple-element.28), channel_id=1, source_target_pairs={{0,1},{1,2},{2,3},{3,4},{4,5},{5,6},{6,7},{8,9},{9,10},{10,11},{11... | collective-permute-start | bytes 34568 | tf_op jit(solution)/shard_map/ppermute | solution.py:16
  225.5 18.7 %collective-permute-start.7 = (bf16[18,1,320]{2,0,1:T(8,128)(2,1)S(1)}, bf16[18,1,320]{2,0,1:T(8,128)(2,1)S(1)}, u32[]{:S(2)}, u32[]{:S(2)}) collective-permute-start(bf16[18,1,320]{2,0,1:T(8,128)(2,1)S(1)} %get-tuple-element.29), channel_id=1, source_target_pairs={{1,0},{2,1},{3,2},{4,3},{5,4},{6,5},{7,6},{9,8},{10,9},{11,10},{12... | collective-permute-start | bytes 34568 | tf_op jit(solution)/shard_map/ppermute | solution.py:19
  245.0 1.6 copy-start.16
  250.5 0.7 copy-start.10
  257.2 2.0 copy-start.3
  257.3 1.9 copy-start.17
  259.2 5.7 %copy-start.1 = (bf16[3,3,320,320]{3,2,1,0:T(8,128)(2,1)S(1)}, bf16[3,3,320,320]{3,2,1,0:T(8,128)(2,1)}, u32[]{:S(2)}) copy-start(bf16[3,3,320,320]{3,2,1,0:T(8,128)(2,1)} %param.20) | copy-start | bytes 5529604
Sparse Core Ops, SparseCore 0:
  18.1 30.1 all-gather.2
  138.0 32.4 all-gather.4
where the time goes:
time: 273 us; the launch traced here: 272 us
  blocking collectives  91.3 us (33%)
  local copies, waits for them, and re-layouts  45.5 us (17%)
  waiting for transfers between devices  45.2 us (17%)
  starting transfers between devices  41.2 us (15%)
  matrix products  18.1 us (7%)
  other arithmetic  15.6 us (6%)
  between operations  14.7 us (5%)
    psum x1, blocking collectives, body(): sums, squares = lax.psum((sums, squares), ('rows', 'cols'))  42 us
    psum x1, blocking collectives, body(): sums_two, squares_two = lax.psum((sums_two, squares_two), ('rows', 'cols'))  37.3 us
    ppermute x6, starting transfers between devices, extended(): lax.ppermute(lax.slice_in_dim(block, block.shape[dim] - width, None, axis...  27.5 us
    all_gather x1, waiting for transfers between devices, body(): whole = lax.all_gather(edged_tile, 'cols', axis=1, tiled=True)  27.1 us
    ppermute x6, waiting for transfers between devices, extended(): lax.ppermute(lax.slice_in_dim(block, 0, width, axis=dim), axis, backward)  18 us
    unnamed x52, local copies, waits for them, and re-layouts  16.6 us
    ppermute x6, starting transfers between devices, extended(): lax.ppermute(lax.slice_in_dim(block, 0, width, axis=dim), axis, backward)  13.7 us
    conv_general_dilated x3, matrix products, conv_valid(): lax.conv_general_dilated(padded[None], kernel, (1, 1), 'VALID', dimension...  12.5 us
  transfers between devices with their start and end apart: 14, of which 8 were waited for; matrix products, arithmetic and copies ran while one was open for 14% of the time, Pallas kernels for 0%

commit v1 on v0

--- a/solution.py
+++ b/solution.py
@@ -94,7 +94,9 @@
     padded = extended(act1, (("rows", 0), ("cols", 1)), 1)
     hid1 = conv_valid(padded, conv1a_w)
     sums_two, squares_two = moments(hid1, width_one)
-    sums_two, squares_two = lax.psum((sums_two, squares_two), ("rows", "cols"))
+    sums_two, squares_two = lax.psum(
+        lax.psum((sums_two, squares_two), axis_name="cols"), axis_name="rows"
+    )
     act2 = normalize(hid1, sums_two, squares_two, count_one, norm1b_g, norm1b_b)
     padded_two = extended(act2, (("rows", 0), ("cols", 1)), 1)
     out1 = (latent1.astype(jnp.float32) + conv_valid(padded_two, conv1b_w) + conv1b_b).astype(

time: 273 us -> 213 us (0.78)
  waiting for transfers between devices: 45.2 us -> 7.74 us
  blocking collectives: 91.3 us -> 70 us
  local copies, waits for them, and re-layouts: 45.5 us -> 39.5 us
  starting transfers between devices: 41.2 us -> 44.8 us
    all_gather x1, waiting for transfers between devices: 27.1 us -> 0.01 us  [body(): whole = lax.all_gather(edged_tile, 'cols', axis=1, tiled=True)]
    psum x2, blocking collectives: 43.3 us -> 18.5 us  [the longest x1 12.7 us: body(): lax.psum((sums_two, squares_two), axis_name='cols')]
    ppermute x6, waiting for transfers between devices: 18 us -> 0.13 us  [extended(): lax.ppermute(lax.slice_in_dim(block, 0, width, axis=dim), axis, backward)]
    ppermute x6, starting transfers between devices: 13.7 us -> 24.6 us  [extended(): lax.ppermute(lax.slice_in_dim(block, 0, width, axis=dim), axis, backward)]
    ppermute x6, waiting for transfers between devices: 0.13 us -> 7.57 us  [extended(): lax.ppermute(lax.slice_in_dim(block, block.shape[dim] - width, None, axis...]
    ppermute x6, starting transfers between devices: 27.5 us -> 20.2 us  [extended(): lax.ppermute(lax.slice_in_dim(block, block.shape[dim] - width, None, axis...]
    unnamed x52, local copies, waits for them, and re-layouts: 16.6 us -> 13.7 us
  transfers between devices with their start and end apart: 14 -> 14, of which waited for: 8 -> 7; matrix products, arithmetic and copies ran while one was open for 14% -> 18% of each run, Pallas kernels for 0% -> 0%
where the time goes in v1:
time: 213 us; the launch traced here: 210 us
  blocking collectives  70 us (33%)
  starting transfers between devices  44.8 us (21%)
  local copies, waits for them, and re-layouts  39.5 us (19%)
  matrix products  18.1 us (8%)
  other arithmetic  15 us (7%)
  between operations  14.7 us (7%)
  waiting for transfers between devices  7.74 us (4%)
    psum x1, blocking collectives, body(): sums, squares = lax.psum((sums, squares), ('rows', 'cols'))  43.3 us
    ppermute x6, starting transfers between devices, extended(): lax.ppermute(lax.slice_in_dim(block, 0, width, axis=dim), axis, backward)  24.6 us
    ppermute x6, starting transfers between devices, extended(): lax.ppermute(lax.slice_in_dim(block, block.shape[dim] - width, None, axis...  20.2 us
    unnamed x52, local copies, waits for them, and re-layouts  13.7 us
    psum x1, blocking collectives, body(): lax.psum((sums_two, squares_two), axis_name='cols')  12.7 us
    conv_general_dilated x3, matrix products, conv_valid(): lax.conv_general_dilated(padded[None], kernel, (1, 1), 'VALID', dimension...  12.5 us
    reshape x1, local copies, waits for them, and re-layouts, folder(): weights = kernel.reshape(9 * count, kernel.shape[3])  9.37 us
    conv_general_dilated x11, local copies, waits for them, and re-layouts, conv_valid(): lax.conv_general_dilated(padded[None], kernel, (1, 1), 'VALID', dimension...  8.87 us
  transfers between devices with their start and end apart: 14, of which 7 were waited for; matrix products, arithmetic and copies ran while one was open for 18% of the time, Pallas kernels for 0%

profile of v1, /device:TPU:3, one launch (start us, length us, event | category | flops | bytes accessed | tf_op | source)
XLA Modules:
  0.0 209.9 jit_solution(1590151642484781470)
XLA Ops:
  7.2 1.2 add_convert_fusion
  8.4 1.9 collective-permute-start.9
  10.4 4.3 %collective-permute-start.8 = (bf16[1,16,1280]{2,1,0:T(8,128)(2,1)S(1)}, bf16[1,16,1280]{2,1,0:T(8,128)(2,1)S(1)}, u32[]{:S(2)}, u32[]{:S(2)}) collective-permute-start(bf16[1,16,1280]{2,1,0:T(8,128)(2,1)S(1)} %get-tuple-element.40), channel_id=1, source_target_pairs={{0,8},{8,16},{16,24},{1,9},{9,17},{17,25},{2,10},{10,18},{18,26},{... | collective-permute-start | bytes 122888 | tf_op jit(solution)/shard_map/ppermute | solution.py:16
  14.7 1.1 collective-permute-done.8
  15.7 0.7 pad_maximum_fusion
  16.5 1.6 convert_reduce_fusion.1
  18.6 43.3 %all-reduce.2 = (f32[32]{0:T(128)S(1)}, f32[32]{0:T(128)S(1)}) all-reduce(f32[32]{0:T(128)S(1)} %reduce_sum.100, f32[32]{0:T(128)S(1)} %reduce_sum.97), channel_id=1, replica_groups=mesh['rows'=4,'cols'=8] {'rows','cols'}, use_global_device_ids=true, to_apply=%region_5.6 | all-reduce | flops 64 | bytes 512 | tf_op jit(solution)/shard_map/psum | solution.py:92
  62.3 1.9 fusion.20
  64.2 0.2 fusion.61
  64.3 1.9 collective-permute-start.1
  66.3 4.3 %collective-permute-start = (bf16[1,64,320]{2,0,1:T(2,128)(2,1)S(1)}, bf16[1,64,320]{2,0,1:T(2,128)(2,1)S(1)}, u32[]{:S(2)}, u32[]{:S(2)}) collective-permute-start(bf16[1,64,320]{2,0,1:T(2,128)(2,1)S(1)} %get-tuple-element.36), channel_id=1, source_target_pairs={{0,8},{8,16},{16,24},{1,9},{9,17},{17,25},{2,10},{10,18},{18,26},{... | collective-permute-start | bytes 122888 | tf_op jit(solution)/shard_map/ppermute | solution.py:16
  70.6 1.6 collective-permute-done
  72.2 4.1 %collective-permute-start.3 = (bf16[18,1,320]{2,0,1:T(8,128)(2,1)S(1)}, bf16[18,1,320]{2,0,1:T(8,128)(2,1)S(1)}, u32[]{:S(2)}, u32[]{:S(2)}) collective-permute-start(bf16[18,1,320]{2,0,1:T(8,128)(2,1)S(1)} %get-tuple-element.33), channel_id=1, source_target_pairs={{1,0},{2,1},{3,2},{4,3},{5,4},{6,5},{7,6},{9,8},{10,9},{11,10},{12... | collective-permute-start | bytes 34568 | tf_op jit(solution)/shard_map/ppermute | solution.py:19
  76.3 3.3 %collective-permute-start.2 = (bf16[18,1,320]{2,0,1:T(8,128)(2,1)S(1)}, bf16[18,1,320]{2,0,1:T(8,128)(2,1)S(1)}, u32[]{:S(2)}, u32[]{:S(2)}) collective-permute-start(bf16[18,1,320]{2,0,1:T(8,128)(2,1)S(1)} %get-tuple-element.32), channel_id=1, source_target_pairs={{0,1},{1,2},{2,3},{3,4},{4,5},{5,6},{6,7},{8,9},{9,10},{10,11},{11... | collective-permute-start | bytes 34568 | tf_op jit(solution)/shard_map/ppermute | solution.py:16
  79.6 0.8 collective-permute-done.2
  80.4 0.7 maximum_bitcast_fusion
  81.2 0.2 pad.9
  81.6 0.3 copy-done.19
  81.9 5.1 %select_reduce_fusion.1 = (f32[320]{0:T(512)S(1)}, f32[320]{0:T(512)S(1)}, f32[16,8,9,320]{3,1,2,0:T(8,128)}) fusion(pred[8,9]{0,1:T(8,128)(4,1)S(1)} %copy-done.19, bf16[3,3,320,320]{3,2,1,0:T(8,128)(2,1)S(1)} %copy-done, bf16[18,1,7,2,320]{4,2,3,0,1:T(8,128)(2,1)S(1)} %slice.100, bf16[18,1,8,9,320]{4,2,3,0,1:T(8,128)(2,1)S(1)} %copy.97), kind=kOutput, calls=%fused_computation.22 | convolution fusion | flops 2128619008 | bytes 4311112 | tf_op jit(solution)/shard_map/conv_general_dilated | solution.py:25
  87.4 12.7 %all-reduce.3 = (f32[32]{0:T(128)S(1)}, f32[32]{0:T(128)S(1)}) all-reduce(f32[32]{0:T(128)S(1)} %reduce_sum.112, f32[32]{0:T(128)S(1)} %reduce_sum.106), channel_id=1, replica_groups=mesh['rows'=4,'cols'=8] {'cols'}, use_global_device_ids=true, to_apply=%region_12.13 | all-reduce | flops 64 | bytes 512 | tf_op jit(solution)/shard_map/psum | solution.py:98
  100.2 1.3 slice-done
  101.5 0.8 copy.113
  102.3 0.4 convert_reduce_fusion
  103.1 8.2 %all-reduce.5 = (f32[32]{0:T(128)S(1)}, f32[32]{0:T(128)S(1)}) all-reduce(f32[32]{0:T(128)S(1)} %reduce_sum.145, f32[32]{0:T(128)S(1)} %reduce_sum.115), channel_id=1, replica_groups=mesh['rows'=4,'cols'=8] {'rows'}, use_global_device_ids=true, to_apply=%region_19.20 | all-reduce | flops 64 | bytes 512 | tf_op jit(solution)/shard_map/psum | solution.py:53
  111.7 3.0 %fusion.11 = bf16[6,128,1280]{2,1,0:T(8,128)(2,1)S(1)} fusion(bf16[6,128,1280]{2,1,0:T(8,128)(2,1)} %all-gather.3.cloned.1.call-done, f32[1280]{0:T(1024)S(1)} %copy-done.6, f32[1280]{0:T(1024)S(1)} %copy-done.7, f32[1280]{0:T(1024)S(1)} %mul.156, f32[1280]{0:T(1024)S(1)} %sub.79, pred[6]{0:T(512)(128)(4,1)S(1)} %compare_and_fusion), kind=kLoop, calls=%fused_computation.20 | loop fusion | flops 10813440 | bytes 3952646 | tf_op jit(solution)/shard_map/jit(_where)/select_n | solution.py:119
  114.7 0.5 pad_bitcast_fusion
  115.3 2.4 %reshape.81 = bf16[6,1,8,17,1280]{4,3,2,0,1:T(8,128)(2,1)} reshape(bf16[6,1,136,1280]{3,2,0,1:T(8,128)(2,1)S(1)} %pad.13) | data formatting | bytes 4177920 | tf_op jit(solution)/shard_map/conv_general_dilated | solution.py:25
  117.7 2.4 %copy.104 = bf16[6,1,8,17,1280]{4,2,3,0,1:T(8,128)(2,1)S(1)} copy(bf16[6,1,8,17,1280]{4,3,2,0,1:T(8,128)(2,1)} %reshape.81) | data formatting | bytes 4177920 | tf_op jit(solution)/shard_map/conv_general_dilated | solution.py:25
  120.2 0.5 copy-done.15
  120.7 3.5 %select_reduce_fusion.3 = (f32[160]{0:T(256)S(1)}, f32[160]{0:T(256)S(1)}, f32[4,8,17,160]{3,1,2,0:T(8,128)S(1)}) fusion(pred[8,17]{0,1:T(8,128)(4,1)S(1)} %copy-done.18, bf16[3,3,1280,160]{2,3,1,0:T(8,128)(2,1)S(1)} %copy-done.15, bf16[6,1,7,2,1280]{4,2,3,0,1:T(8,128)(2,1)S(1)} %slice.109, bf16[6,1,8,17,1280]{4,2,3,0,1:T(8,128)(2,1)S(1)} %copy.104), kind=kOutput, calls=%fused_computation.73 | convolution fusion | flops 2012927744 | bytes 6339976 | tf_op jit(solution)/shard_map/conv_general_dilated | solution.py:25
  124.6 0.2 copy.105
  124.9 0.2 copy.114
  125.1 5.8 %all-reduce.4 = (f32[32]{0:T(128)S(1)}, f32[32]{0:T(128)S(1)}, f32[4]{0:T(128)S(1)}, f32[4]{0:T(128)S(1)}) all-reduce(f32[32]{0:T(128)S(1)} %get-tuple-element.22, f32[32]{0:T(128)S(1)} %get-tuple-element.23, f32[4]{0:T(128)S(1)} %reduce_sum.151, f32[4]{0:T(128)S(1)} %reduce_sum.148), channel_id=1, replica_groups=mesh['rows'=4,'cols'=8] {'rows'}, use_global_device_ids=true, to_apply=%region_13.14 | all-reduce | flops 72 | bytes 576 | tf_op jit(solution)/shard_map/psum | solution.py:97
  131.2 0.2 multiply_convert_fusion.2
  131.5 4.0 %collective-permute-start.11 = (bf16[1,128,160]{1,2,0:T(8,128)(2,1)S(1)}, bf16[1,128,160]{1,2,0:T(8,128)(2,1)S(1)}, u32[]{:S(2)}, u32[]{:S(2)}) collective-permute-start(bf16[1,128,160]{1,2,0:T(8,128)(2,1)S(1)} %get-tuple-element.39), channel_id=1, source_target_pairs={{8,0},{16,8},{24,16},{9,1},{17,9},{25,17},{10,2},{18,10},{26,18},{... | collective-permute-start | bytes 122888 | tf_op jit(solution)/shard_map/ppermute | solution.py:19
  135.5 2.2 %collective-permute-start.10 = (bf16[1,128,160]{1,2,0:T(8,128)(2,1)S(1)}, bf16[1,128,160]{1,2,0:T(8,128)(2,1)S(1)}, u32[]{:S(2)}, u32[]{:S(2)}) collective-permute-start(bf16[1,128,160]{1,2,0:T(8,128)(2,1)S(1)} %get-tuple-element.38), channel_id=1, source_target_pairs={{0,8},{8,16},{16,24},{1,9},{9,17},{17,25},{2,10},{10,18},{18,26},{... | collective-permute-start | bytes 122888 | tf_op jit(solution)/shard_map/ppermute | solution.py:16
  137.7 2.5 %collective-permute-done.10 = bf16[1,128,160]{1,2,0:T(8,128)(2,1)S(1)} collective-permute-done((bf16[1,128,160]{1,2,0:T(8,128)(2,1)S(1)}, bf16[1,128,160]{1,2,0:T(8,128)(2,1)S(1)}, u32[]{:S(2)}, u32[]{:S(2)}) %collective-permute-start.10) | collective-permute-done | bytes 40992 | tf_op jit(solution)/shard_map/ppermute | solution.py:16
  140.2 0.7 pad_maximum_fusion.1
  141.0 3.0 %copy.98 = f32[16,8,9,320]{3,0,2,1:T(8,128)} copy(f32[16,8,9,320]{3,1,2,0:T(8,128)} %get-tuple-element.50) | data formatting | bytes 2949120 | tf_op jit(solution)/shard_map/conv_general_dilated | solution.py:25
  144.4 2.1 multiply_convert_fusion.1
  146.7 1.9 collective-permute-start.5
  148.6 4.3 %collective-permute-start.4 = (bf16[1,64,320]{2,0,1:T(2,128)(2,1)S(1)}, bf16[1,64,320]{2,0,1:T(2,128)(2,1)S(1)}, u32[]{:S(2)}, u32[]{:S(2)}) collective-permute-start(bf16[1,64,320]{2,0,1:T(2,128)(2,1)S(1)} %get-tuple-element.34), channel_id=1, source_target_pairs={{0,8},{8,16},{16,24},{1,9},{9,17},{17,25},{2,10},{10,18},{18,26},{... | collective-permute-start | bytes 122888 | tf_op jit(solution)/shard_map/ppermute | solution.py:16
  152.9 1.6 collective-permute-done.4
  154.5 10.7 %collective-permute-start.7 = (bf16[18,1,320]{2,0,1:T(8,128)(2,1)S(1)}, bf16[18,1,320]{2,0,1:T(8,128)(2,1)S(1)}, u32[]{:S(2)}, u32[]{:S(2)}) collective-permute-start(bf16[18,1,320]{2,0,1:T(8,128)(2,1)S(1)} %get-tuple-element.31), channel_id=1, source_target_pairs={{1,0},{2,1},{3,2},{4,3},{5,4},{6,5},{7,6},{9,8},{10,9},{11,10},{12... | collective-permute-start | bytes 34568 | tf_op jit(solution)/shard_map/ppermute | solution.py:19
  165.3 1.9 collective-permute-start.6
  167.2 5.4 %copy.111 = bf16[3,3,1280,160]{2,1,0,3:T(4,128)(2,1)} copy(bf16[3,3,1280,160]{2,3,1,0:T(8,128)(2,1)S(1)} %copy-done.4) | data formatting | bytes 7372800 | tf_op args[15]
  172.6 9.4 %reshape.109 = bf16[11520,160,1]{0,1,2:T(8,128)(2,1)} reshape(bf16[3,3,1280,160]{2,1,0,3:T(4,128)(2,1)} %copy.111) | data formatting | bytes 7372800 | tf_op jit(solution)/shard_map/reshape | solution.py:63
  181.9 0.7 maximum_bitcast_fusion.1
  182.7 0.2 pad.11
  183.1 1.2 copy-done.16
  184.3 3.8 %convolution_select_fusion = f32[16,8,9,320]{3,1,2,0:T(8,128)S(1)} fusion(bf16[3,3,320,320]{3,2,1,0:T(8,128)(2,1)S(1)} %copy-done.16, bf16[18,1,7,2,320]{4,2,3,0,1:T(8,128)(2,1)S(1)} %slice.104, bf16[18,1,8,9,320]{4,2,3,0,1:T(8,128)(2,1)S(1)} %copy.100, pred[8,9]{0,1:T(8,128)(4,1)S(1)} %copy-done.19), kind=kOutput, calls=%fused_computation.42 | convolution fusion | flops 2126776320 | bytes 4308552 | tf_op jit(solution)/shard_map/conv_general_dilated | solution.py:25
  188.2 0.3 copy.101
  188.5 0.8 copy-done.2
  189.3 0.6 fusion.23
  189.9 1.1 copy.112
  190.9 2.7 %copy.107 = bf16[6,128,1280]{2,1,0:T(8,128)(2,1)S(1)} copy(bf16[6,128,1280]{1,2,0:T(8,128)(2,1)} %all-gather.5.cloned.1.call-done) | data formatting | bytes 3932160 | tf_op jit(solution)/shard_map/all_gather | solution.py:125
  193.6 0.3 slice_dynamic-update-slice_fusion.8
  194.0 0.3 slice_dynamic-update-slice_fusion.7
  194.3 0.3 slice_dynamic-update-slice_fusion.6
  194.7 0.3 slice_dynamic-update-slice_fusion.5
  195.0 0.3 slice_dynamic-update-slice_fusion.4
  195.5 0.3 slice_dynamic-update-slice_fusion.3
  195.8 1.6 copy-done.5
  197.4 5.7 %fusion.45 = bf16[4,128,160]{1,2,0:T(8,128)(2,1)} fusion(bf16[4,128,11520]{2,1,0:T(8,128)(2,1)S(1)} %slice_dynamic-update-slice_fusion.3, bf16[11520,160,1]{0,1,2:T(8,128)(2,1)S(1)} %copy-done.5, f32[160]{0:T(256)S(1)} %copy-done.17, bf16[4,128,1280]{1,2,0:T(8,128)(2,1)} %copy-done.3, s32[]{:T(128)S(6)} %select_n.7), kind=kOutput, calls=%fused_computation.69 | convolution fusion | flops 1887764480 | bytes 15811204 | tf_op jit(solution)/shard_map/dot_general | solution.py:64
  (101 shorter events, 4.5 us)
Async XLA Ops:
  7.2 74.4 %copy-start = (bf16[3,3,320,320]{3,2,1,0:T(8,128)(2,1)S(1)}, bf16[3,3,320,320]{3,2,1,0:T(8,128)(2,1)}, u32[]{:S(2)}) copy-start(bf16[3,3,320,320]{3,2,1,0:T(8,128)(2,1)} %param.20) | copy-start | bytes 5529604
  7.2 55.1 %copy-start.8 = (f32[320]{0:T(512)S(1)}, f32[320]{0:T(512)}, u32[]{:S(2)}) copy-start(f32[320]{0:T(512)} %param.19) | copy-start | bytes 3844
  7.2 55.1 %copy-start.9 = (f32[320]{0:T(512)S(1)}, f32[320]{0:T(512)}, u32[]{:S(2)}) copy-start(f32[320]{0:T(512)} %param.18) | copy-start | bytes 3844
  7.2 93.0 %all-gather.3.cloned.1.call-start = ((), (), s32[]{:S(2)}) async-start(), calls=%async_computation | async-start | bytes 2211840 | tf_op jit(solution)/shard_map/all_gather | solution.py:113
  8.4 6.2 %collective-permute-start.9 = (bf16[1,16,1280]{2,1,0:T(8,128)(2,1)S(1)}, bf16[1,16,1280]{2,1,0:T(8,128)(2,1)S(1)}, u32[]{:S(2)}, u32[]{:S(2)}) collective-permute-start(bf16[1,16,1280]{2,1,0:T(8,128)(2,1)S(1)} %get-tuple-element.41), channel_id=1, source_target_pairs={{8,0},{16,8},{24,16},{9,1},{17,9},{25,17},{10,2},{18,10},{26,18},{... | collective-permute-start | bytes 122888 | tf_op jit(solution)/shard_map/ppermute | solution.py:19
  10.4 5.3 %collective-permute-start.8 = (bf16[1,16,1280]{2,1,0:T(8,128)(2,1)S(1)}, bf16[1,16,1280]{2,1,0:T(8,128)(2,1)S(1)}, u32[]{:S(2)}, u32[]{:S(2)}) collective-permute-start(bf16[1,16,1280]{2,1,0:T(8,128)(2,1)S(1)} %get-tuple-element.40), channel_id=1, source_target_pairs={{0,8},{8,16},{16,24},{1,9},{9,17},{17,25},{2,10},{10,18},{18,26},{... | collective-permute-start | bytes 122888 | tf_op jit(solution)/shard_map/ppermute | solution.py:16
  16.5 174.5 %all-gather.5.cloned.1.call-start = ((), (), s32[]{:S(2)}) async-start(), calls=%async_computation.1 | async-start | bytes 2211840 | tf_op jit(solution)/shard_map/all_gather | solution.py:125
  64.3 6.3 %collective-permute-start.1 = (bf16[1,64,320]{2,0,1:T(2,128)(2,1)S(1)}, bf16[1,64,320]{2,0,1:T(2,128)(2,1)S(1)}, u32[]{:S(2)}, u32[]{:S(2)}) collective-permute-start(bf16[1,64,320]{2,0,1:T(2,128)(2,1)S(1)} %get-tuple-element.37), channel_id=1, source_target_pairs={{8,0},{16,8},{24,16},{9,1},{17,9},{25,17},{10,2},{18,10},{26,18},{... | collective-permute-start | bytes 122888 | tf_op jit(solution)/shard_map/ppermute | solution.py:19
  66.3 5.9 %collective-permute-start = (bf16[1,64,320]{2,0,1:T(2,128)(2,1)S(1)}, bf16[1,64,320]{2,0,1:T(2,128)(2,1)S(1)}, u32[]{:S(2)}, u32[]{:S(2)}) collective-permute-start(bf16[1,64,320]{2,0,1:T(2,128)(2,1)S(1)} %get-tuple-element.36), channel_id=1, source_target_pairs={{0,8},{8,16},{16,24},{1,9},{9,17},{17,25},{2,10},{10,18},{18,26},{... | collective-permute-start | bytes 122888 | tf_op jit(solution)/shard_map/ppermute | solution.py:16
  72.2 7.4 %collective-permute-start.3 = (bf16[18,1,320]{2,0,1:T(8,128)(2,1)S(1)}, bf16[18,1,320]{2,0,1:T(8,128)(2,1)S(1)}, u32[]{:S(2)}, u32[]{:S(2)}) collective-permute-start(bf16[18,1,320]{2,0,1:T(8,128)(2,1)S(1)} %get-tuple-element.33), channel_id=1, source_target_pairs={{1,0},{2,1},{3,2},{4,3},{5,4},{6,5},{7,6},{9,8},{10,9},{11,10},{12... | collective-permute-start | bytes 34568 | tf_op jit(solution)/shard_map/ppermute | solution.py:19
  76.3 4.2 %collective-permute-start.2 = (bf16[18,1,320]{2,0,1:T(8,128)(2,1)S(1)}, bf16[18,1,320]{2,0,1:T(8,128)(2,1)S(1)}, u32[]{:S(2)}, u32[]{:S(2)}) collective-permute-start(bf16[18,1,320]{2,0,1:T(8,128)(2,1)S(1)} %get-tuple-element.32), channel_id=1, source_target_pairs={{0,1},{1,2},{2,3},{3,4},{4,5},{5,6},{6,7},{8,9},{9,10},{10,11},{11... | collective-permute-start | bytes 34568 | tf_op jit(solution)/shard_map/ppermute | solution.py:16
  81.2 0.7 copy-start.19
  100.2 1.3 slice-start
  101.5 10.2 %copy-start.6 = (f32[1280]{0:T(1024)S(1)}, f32[1280]{0:T(1024)}, u32[]{:S(2)}) copy-start(f32[1280]{0:T(1024)} %param.28) | copy-start | bytes 15364
  101.5 10.2 %copy-start.7 = (f32[1280]{0:T(1024)S(1)}, f32[1280]{0:T(1024)}, u32[]{:S(2)}) copy-start(f32[1280]{0:T(1024)} %param.27) | copy-start | bytes 15364
  102.3 9.3 %copy-start.3 = (bf16[4,128,1280]{1,2,0:T(8,128)(2,1)}, bf16[4,128,1280]{1,2,0:T(8,128)(2,1)S(1)}, u32[]{:S(2)}) copy-start(bf16[4,128,1280]{1,2,0:T(8,128)(2,1)S(1)} %copy.113) | copy-start | bytes 3932164
  117.7 2.9 %copy-start.15 = (bf16[3,3,1280,160]{2,3,1,0:T(8,128)(2,1)S(1)}, bf16[3,3,1280,160]{2,3,1,0:T(8,128)(2,1)}, u32[]{:S(2)}) copy-start(bf16[3,3,1280,160]{2,3,1,0:T(8,128)(2,1)} %param.29) | copy-start | bytes 11059204
  117.7 2.9 %copy-start.18 = (pred[8,17]{0,1:T(8,128)(4,1)S(1)}, pred[8,17]{0,1:T(8,128)(4,1)}, u32[]{:S(2)}) copy-start(pred[8,17]{0,1:T(8,128)(4,1)} %constant.75) | copy-start | bytes 412
  124.2 7.1 %copy-start.13 = (f32[160]{0:T(256)S(1)}, f32[160]{0:T(256)}, u32[]{:S(2)}) copy-start(f32[160]{0:T(256)} %param.31) | copy-start | bytes 1924
  124.2 7.0 %copy-start.14 = (f32[160]{0:T(256)S(1)}, f32[160]{0:T(256)}, u32[]{:S(2)}) copy-start(f32[160]{0:T(256)} %param.30) | copy-start | bytes 1924
  131.5 6.2 %collective-permute-start.11 = (bf16[1,128,160]{1,2,0:T(8,128)(2,1)S(1)}, bf16[1,128,160]{1,2,0:T(8,128)(2,1)S(1)}, u32[]{:S(2)}, u32[]{:S(2)}) collective-permute-start(bf16[1,128,160]{1,2,0:T(8,128)(2,1)S(1)} %get-tuple-element.39), channel_id=1, source_target_pairs={{8,0},{16,8},{24,16},{9,1},{17,9},{25,17},{10,2},{18,10},{26,18},{... | collective-permute-start | bytes 122888 | tf_op jit(solution)/shard_map/ppermute | solution.py:19
  135.5 9.0 %copy-start.10 = (f32[320]{0:T(512)S(1)}, f32[320]{0:T(512)}, u32[]{:S(2)}) copy-start(f32[320]{0:T(512)} %param.22) | copy-start | bytes 3844
  135.5 8.9 %copy-start.11 = (f32[320]{0:T(512)S(1)}, f32[320]{0:T(512)}, u32[]{:S(2)}) copy-start(f32[320]{0:T(512)} %param.21) | copy-start | bytes 3844
  135.5 4.7 %collective-permute-start.10 = (bf16[1,128,160]{1,2,0:T(8,128)(2,1)S(1)}, bf16[1,128,160]{1,2,0:T(8,128)(2,1)S(1)}, u32[]{:S(2)}, u32[]{:S(2)}) collective-permute-start(bf16[1,128,160]{1,2,0:T(8,128)(2,1)S(1)} %get-tuple-element.38), channel_id=1, source_target_pairs={{0,8},{8,16},{16,24},{1,9},{9,17},{17,25},{2,10},{10,18},{18,26},{... | collective-permute-start | bytes 122888 | tf_op jit(solution)/shard_map/ppermute | solution.py:16
  144.4 22.8 %copy-start.4 = (bf16[3,3,1280,160]{2,3,1,0:T(8,128)(2,1)S(1)}, bf16[3,3,1280,160]{2,3,1,0:T(8,128)(2,1)}, u32[]{:S(2)}) copy-start(bf16[3,3,1280,160]{2,3,1,0:T(8,128)(2,1)} %param.32) | copy-start | bytes 11059204
  146.7 6.3 %collective-permute-start.5 = (bf16[1,64,320]{2,0,1:T(2,128)(2,1)S(1)}, bf16[1,64,320]{2,0,1:T(2,128)(2,1)S(1)}, u32[]{:S(2)}, u32[]{:S(2)}) collective-permute-start(bf16[1,64,320]{2,0,1:T(2,128)(2,1)S(1)} %get-tuple-element.35), channel_id=1, source_target_pairs={{8,0},{16,8},{24,16},{9,1},{17,9},{25,17},{10,2},{18,10},{26,18},{... | collective-permute-start | bytes 122888 | tf_op jit(solution)/shard_map/ppermute | solution.py:19
  148.6 5.9 %collective-permute-start.4 = (bf16[1,64,320]{2,0,1:T(2,128)(2,1)S(1)}, bf16[1,64,320]{2,0,1:T(2,128)(2,1)S(1)}, u32[]{:S(2)}, u32[]{:S(2)}) collective-permute-start(bf16[1,64,320]{2,0,1:T(2,128)(2,1)S(1)} %get-tuple-element.34), channel_id=1, source_target_pairs={{0,8},{8,16},{16,24},{1,9},{9,17},{17,25},{2,10},{10,18},{18,26},{... | collective-permute-start | bytes 122888 | tf_op jit(solution)/shard_map/ppermute | solution.py:16
  154.5 27.4 %collective-permute-start.7 = (bf16[18,1,320]{2,0,1:T(8,128)(2,1)S(1)}, bf16[18,1,320]{2,0,1:T(8,128)(2,1)S(1)}, u32[]{:S(2)}, u32[]{:S(2)}) collective-permute-start(bf16[18,1,320]{2,0,1:T(8,128)(2,1)S(1)} %get-tuple-element.31), channel_id=1, source_target_pairs={{1,0},{2,1},{3,2},{4,3},{5,4},{6,5},{7,6},{9,8},{10,9},{11,10},{12... | collective-permute-start | bytes 34568 | tf_op jit(solution)/shard_map/ppermute | solution.py:19
  165.3 16.7 %collective-permute-start.6 = (bf16[18,1,320]{2,0,1:T(8,128)(2,1)S(1)}, bf16[18,1,320]{2,0,1:T(8,128)(2,1)S(1)}, u32[]{:S(2)}, u32[]{:S(2)}) collective-permute-start(bf16[18,1,320]{2,0,1:T(8,128)(2,1)S(1)} %get-tuple-element.30), channel_id=1, source_target_pairs={{0,1},{1,2},{2,3},{3,4},{4,5},{5,6},{6,7},{8,9},{9,10},{10,11},{11... | collective-permute-start | bytes 34568 | tf_op jit(solution)/shard_map/ppermute | solution.py:16
  182.7 1.6 copy-start.16
  188.1 1.1 copy-start.2
  188.1 1.1 copy-start.12
  195.3 2.0 copy-start.5
  195.4 1.9 copy-start.17
  197.4 5.7 %copy-start.1 = (bf16[3,3,320,320]{3,2,1,0:T(8,128)(2,1)S(1)}, bf16[3,3,320,320]{3,2,1,0:T(8,128)(2,1)}, u32[]{:S(2)}) copy-start(bf16[3,3,320,320]{3,2,1,0:T(8,128)(2,1)} %param.20) | copy-start | bytes 5529604
Sparse Core Ops, SparseCore 0:
  16.6 32.3 all-gather.2
  141.1 32.8 all-gather.4
